TPU v7x, 32 devices: a whole 2x2x4 slice. The times are simulated.
32 devices in a mesh: dp: 8 (over z, y), blk: 4 (over x, core).
Axes of the slice: x: 2, y: 2, z: 4, core: 2. Of those that a mesh axis runs over, the one named last changes fastest.
Arguments:
- tokens: bfloat16 [4096, 4096], P(('dp', 'blk')), may hold values from -6 to 6
- gate_projection_weight: bfloat16 [4096, 7168], P(None, 'blk'), may hold values from -0.09375 to 0.09375
- up_projection_weight: bfloat16 [4096, 7168], P('dp', 'blk'), may hold values from -0.09375 to 0.09375
- down_projection_weight: bfloat16 [7168, 4096], P('blk', 'dp'), may hold values from -0.0625 to 0.0625
- router_projection_weight: bfloat16 [4096, 8], replicated, may hold values from -0.09375 to 0.09375
- adapter_down_factors: bfloat16 [4096, 128], replicated, may hold values from -0.09375 to 0.09375
- adapter_up_factors: bfloat16 [128, 4096], replicated, may hold values from -1.5 to 1.5
- routes: int32 [4096, 2], P(('dp', 'blk')), may hold values from 0 to 7, all different within a row
- padding_token_mask: int32 [4096], P(('dp', 'blk')), may hold values 0 or 1
- cotangent: bfloat16 [4096, 4096], P(('dp', 'blk')), may hold values from -6 to 6
Outputs:
- layer_out: bfloat16 [4096, 4096], P(('dp', 'blk'))
- grad_down: float32 [4096, 128], replicated
- grad_up: float32 [128, 4096], replicated
Inputs may be any that keep to these rules, and one draw needn't show every extreme that they name: `routes`: the two experts of a token differ.
All inputs are finite; a program needn't handle non-finite values. No bound on the sum of `padding_token_mask` on one device may be relied on, other than what follows from the above.
Results may differ from a plain program's by a relative error of at most 0.0075.
Values may be sent and summed in bfloat16 or wider, within the bound.
A program may use at most 192 MiB of HBM per device.

v0:
```python
import jax
import jax.numpy as jnp
from jax import lax
from jax.sharding import PartitionSpec as P


def shards(
    tokens,
    gate_projection_weight,
    up_projection_weight,
    down_projection_weight,
    router_projection_weight,
    adapter_down_factors,
    adapter_up_factors,
    routes,
    padding_token_mask,
    cotangent,
):
    grouped = lax.all_gather(tokens, "blk", axis=0, tiled=True)
    gate_act = jnp.dot(grouped, gate_projection_weight, preferred_element_type=jnp.float32)
    up_act = jnp.dot(
        grouped,
        lax.all_gather(up_projection_weight, "dp", axis=0, tiled=True),
        preferred_element_type=jnp.float32,
    )
    down_full = lax.all_gather(down_projection_weight, "dp", axis=1, tiled=True)
    hidden = (jax.nn.silu(gate_act) * up_act).astype(jnp.bfloat16)
    part = jnp.dot(hidden, down_full, preferred_element_type=jnp.float32)
    part = lax.optimization_barrier(part.astype(jnp.bfloat16))
    base = lax.psum_scatter(
        part.astype(jnp.float32).astype(jnp.bfloat16), "blk", scatter_dimension=0, tiled=True
    ).astype(jnp.float32)
    expert_list = router_projection_weight.shape[1]
    rank_index = adapter_down_factors.shape[1] // expert_list
    logits = jnp.dot(tokens, router_projection_weight, preferred_element_type=jnp.float32)
    experts_iota = jnp.arange(expert_list, dtype=jnp.int32)[None, :]
    first_hot = (routes[:, 0:1] == experts_iota).astype(jnp.float32)
    second_hot = (routes[:, 1:2] == experts_iota).astype(jnp.float32)
    first_logit = jnp.sum(logits * first_hot, axis=1, keepdims=True)
    second_logit = jnp.sum(logits * second_hot, axis=1, keepdims=True)
    weight_first = jax.nn.sigmoid(first_logit - second_logit)
    coeff = weight_first * first_hot + (1.0 - weight_first) * second_hot
    coeff_wide = jnp.repeat(coeff, rank_index, axis=1)
    low_rank_state = jnp.dot(tokens, adapter_down_factors, preferred_element_type=jnp.float32)
    scaled_output = (low_rank_state * coeff_wide).astype(jnp.bfloat16)
    adapter_delta = jnp.dot(scaled_output, adapter_up_factors, preferred_element_type=jnp.float32)
    layer_out = (base + adapter_delta).astype(jnp.bfloat16)
    masked_tokens = cotangent * padding_token_mask[:, None].astype(jnp.bfloat16)
    low_rank_gradient = lax.dot_general(
        masked_tokens,
        adapter_up_factors,
        (((1,), (1,)), ((), ())),
        preferred_element_type=jnp.float32,
    )
    dlow = (low_rank_gradient * coeff_wide).astype(jnp.bfloat16)
    local_live = jnp.sum(padding_token_mask.astype(jnp.float32))
    local_up = lax.dot_general(
        scaled_output, masked_tokens, (((0,), (0,)), ((), ())), preferred_element_type=jnp.float32
    )
    local_down = lax.dot_general(
        tokens, dlow, (((0,), (0,)), ((), ())), preferred_element_type=jnp.float32
    )
    summed_down, summed_up, live_total = lax.psum((local_down, local_up, local_live), ("dp", "blk"))
    inverse = 1.0 / jnp.maximum(live_total, 1.0)
    grad_down = summed_down * inverse
    grad_up = summed_up * inverse
    return (layer_out, grad_down, grad_up)


def solution(mesh):
    return jax.shard_map(
        shards,
        mesh=mesh,
        in_specs=(
            P(("dp", "blk"), None),
            P(None, "blk"),
            P("dp", "blk"),
            P("blk", "dp"),
            P(),
            P(),
            P(),
            P(("dp", "blk"), None),
            P(("dp", "blk")),
            P(("dp", "blk"), None),
        ),
        out_specs=(P(("dp", "blk"), None), P(), P()),
        check_vma=False,
    )
```

profile of v0, /device:TPU:0, one launch (start us, length us, event | category | flops | bytes accessed | tf_op | source)
XLA Modules:
  0.0 549.2 jit_solution(12669758104570332105)
XLA Ops:
  8.1 0.0 all-gather.4.cloned.1.call-start
  8.1 0.7 all-gather.4.cloned.1.call-update
  8.8 0.0 all-gather.8.cloned.1.call-start
  8.8 0.7 all-gather.8.cloned.1.call-update
  9.5 0.0 all-gather.6.cloned.1.call-start
  9.6 0.7 all-gather.6.cloned.1.call-update
  10.3 0.0 all-reduce.3.cloned.1.call-start
  10.4 0.4 select_reduce_fusion
  10.8 0.1 copy.15
  10.9 1.6 fusion.2
  12.6 1.8 fusion.4
  14.4 2.7 convolution_bitcast_fusion
  17.2 0.2 reduce-scatter.2.cloned.1.call-start
  17.4 30.6 %all-gather.4.cloned.1.call-done = bf16[512,4096]{1,0:T(8,128)(2,1)} async-done(((bf16[128,4096]{1,0:T(8,128)(2,1)}), bf16[512,4096]{1,0:T(8,128)(2,1)}) %all-gather.4.cloned.1.call-update) | async-done | bytes 4194320 | tf_op jit(solution)/shard_map/all_gather | solution.py:19
  48.0 14.8 %fusion.12 = f32[512,1792]{1,0:T(8,128)} fusion(bf16[512,4096]{1,0:T(8,128)(2,1)} %all-gather.4.cloned.1.call-done, bf16[4096,1792]{1,0:T(8,128)(2,1)} %param.11), kind=kOutput, calls=%fused_computation.28 | convolution fusion | flops 7516192768 | bytes 22544384 | tf_op jit(solution)/shard_map/dot_general | solution.py:20
  62.7 195.0 %all-gather.8.cloned.1.call-done = bf16[1792,4096]{1,0:T(8,128)(2,1)} async-done(((bf16[1792,512]{1,0:T(8,128)(2,1)}), bf16[1792,4096]{1,0:T(8,128)(2,1)}) %all-gather.8.cloned.1.call-update) | async-done | bytes 14680080 | tf_op jit(solution)/shard_map/all_gather | solution.py:26
  257.7 204.7 %all-gather.6.cloned.1.call-done = bf16[4096,1792]{1,0:T(8,128)(2,1)} async-done(((bf16[512,1792]{1,0:T(8,128)(2,1)}), bf16[4096,1792]{1,0:T(8,128)(2,1)}) %all-gather.6.cloned.1.call-update) | async-done | bytes 14680080 | tf_op jit(solution)/shard_map/all_gather | solution.py:23
  462.4 29.0 %convolution_convert_fusion = bf16[512,4096]{1,0:T(8,128)(2,1)} fusion(bf16[1792,4096]{1,0:T(8,128)(2,1)} %all-gather.8.cloned.1.call-done, f32[512,1792]{1,0:T(8,128)} %fusion.12, bf16[512,4096]{1,0:T(8,128)(2,1)} %all-gather.4.cloned.1.call-done, bf16[4096,1792]{1,0:T(8,128)(2,1)} %all-gather.6.cloned.1.call-done), kind=kOutput, calls=%fused_computation | convolution fusion | flops 15039987712 | bytes 41418752 | tf_op jit(solution)/shard_map/dot_general | solution.py:28
  491.4 0.6 convert_reduce_fusion
  492.0 40.0 %psum.22 = f32[]{:T(128)} all-reduce(f32[]{:T(128)} %convert_reduce_fusion), channel_id=1, replica_groups=mesh['dp'=8,'blk'=4] {'dp','blk'}, use_global_device_ids=true, to_apply=%region_5.6 | all-reduce | flops 1 | bytes 8 | tf_op jit(solution)/shard_map/psum | solution.py:63
  532.7 1.8 broadcast_multiply_fusion.1
  534.5 1.8 copy.16
  536.3 3.1 broadcast_multiply_fusion
  539.4 2.6 fusion
  (21 shorter events, 0.1 us)
Async XLA Ops:
  8.0 6.4 %copy-start = (bf16[128,4096]{1,0:T(8,128)(2,1)S(1)}, bf16[128,4096]{1,0:T(8,128)(2,1)}, u32[]{:S(2)}) copy-start(bf16[128,4096]{1,0:T(8,128)(2,1)} %param.16) | copy-start | bytes 3145732
  8.0 2.3 copy-start.1
  8.0 2.3 copy-start.4
  8.0 2.3 copy-start.3
  8.0 2.9 copy-start.5
  8.1 39.9 %all-gather.4.cloned.1.call-start = ((), (), s32[]{:S(2)}) async-start(), calls=%async_computation.1 | async-start | bytes 5242880 | tf_op jit(solution)/shard_map/all_gather | solution.py:19
  8.8 3.8 copy-start.2
  8.8 248.9 %all-gather.8.cloned.1.call-start = ((), (), s32[]{:S(2)}) async-start(), calls=%async_computation.3 | async-start | bytes 16515072 | tf_op jit(solution)/shard_map/all_gather | solution.py:26
  9.5 452.8 %all-gather.6.cloned.1.call-start = ((), (), s32[]{:S(2)}) async-start(), calls=%async_computation.2 | async-start | bytes 16515072 | tf_op jit(solution)/shard_map/all_gather | solution.py:23
  10.3 522.5 %all-reduce.3.cloned.1.call-start = ((), (), s32[]{:S(2)}) async-start(), calls=%async_computation.5 | async-start | bytes 8388608 | tf_op jit(solution)/shard_map/psum | solution.py:63
  17.2 522.3 %reduce-scatter.2.cloned.1.call-start = ((), (), s32[]{:S(2)}) async-start(), calls=%async_computation.4 | async-start | bytes 5242880 | tf_op jit(solution)/shard_map/reduce_scatter | solution.py:30
Sparse Core Ops, SparseCore 0:
  10.4 37.5 all-gather.3
  50.0 207.6 all-gather.7
  259.9 202.4 all-gather.5
  491.5 44.3 reduce-scatter.1
Sparse Core Ops, SparseCore 1:
  17.2 482.6 all-reduce.2
where the time goes:
time: 550 us; the launch traced here: 549 us
  waiting for transfers between devices  432 us (79%)
  matrix products  52.9 us (10%)
  blocking collectives  40 us (7%)
  between operations  16.1 us (3%)
    all_gather x1, waiting for transfers between devices, shards(): lax.all_gather(up_projection_weight, 'dp', axis=0, tiled=True)  205 us
    all_gather x1, waiting for transfers between devices, shards(): down_full = lax.all_gather(down_projection_weight, 'dp', axis=1, tiled=True)  195 us
    psum x1, blocking collectives, shards(): lax.psum((local_down, local_up, local_live), ('dp', 'blk'))  40 us
    all_gather x1, waiting for transfers between devices, shards(): grouped = lax.all_gather(tokens, 'blk', axis=0, tiled=True)  30.6 us
    dot_general x1, matrix products, shards(): part = jnp.dot(hidden, down_full, preferred_element_type=jnp.float32)  29 us
    dot_general x1, matrix products, shards(): jnp.dot(grouped, gate_projection_weight, preferred_element_type=jnp.float32)  14.8 us
  transfers between devices with their start and end apart: 5, of which 3 were waited for; matrix products, arithmetic and copies ran while one was open for 11% of the time, Pallas kernels for 0%

commit v1 on v0

--- a/solution.py
+++ b/solution.py
@@ -2,6 +2,11 @@
 import jax.numpy as jnp
 from jax import lax
 from jax.sharding import PartitionSpec as P
+
+
+def one_after_other(x, axis_one, axis_two):
+    inner = lax.psum(x, axis_one)
+    return lax.psum(inner, axis_two)
 
 
 def shards(
@@ -60,7 +65,9 @@
     local_down = lax.dot_general(
         tokens, dlow, (((0,), (0,)), ((), ())), preferred_element_type=jnp.float32
     )
-    summed_down, summed_up, live_total = lax.psum((local_down, local_up, local_live), ("dp", "blk"))
+    summed_down, summed_up, live_total = one_after_other(
+        (local_down, local_up, local_live), "blk", "dp"
+    )
     inverse = 1.0 / jnp.maximum(live_total, 1.0)
     grad_down = summed_down * inverse
     grad_up = summed_up * inverse

time: 550 us -> 762 us (1.39)
  waiting for transfers between devices: 432 us -> 655 us
  blocking collectives: 40 us -> 27 us
    psum x1 -> x2, waiting for transfers between devices: 0.03 us -> 186 us  [the longest x1 100 us: one_after_other(): return lax.psum(inner, axis_two)]
    reduce_scatter x1, waiting for transfers between devices: 0.01 us -> 39.3 us  [shards(): lax.psum_scatter(part.astype(jnp.float32).astype(jnp.bfloat16), 'blk', sc...]
    psum x1 -> x2, blocking collectives: 40 us -> 27 us  [the longest x1 20.1 us: one_after_other(): return lax.psum(inner, axis_two)]
  transfers between devices with their start and end apart: 5 -> 6, of which waited for: 3 -> 6; matrix products, arithmetic and copies ran while one was open for 11% -> 7% of each run, Pallas kernels for 0% -> 0%
where the time goes in v1:
time: 762 us; the launch traced here: 761 us
  waiting for transfers between devices  655 us (86%)
  matrix products  54.8 us (7%)
  blocking collectives  27 us (4%)
  between operations  14.9 us (2%)
    all_gather x1, waiting for transfers between devices, shards(): lax.all_gather(up_projection_weight, 'dp', axis=0, tiled=True)  202 us
    all_gather x1, waiting for transfers between devices, shards(): down_full = lax.all_gather(down_projection_weight, 'dp', axis=1, tiled=True)  189 us
    psum x1, waiting for transfers between devices, one_after_other(): return lax.psum(inner, axis_two)  100 us
    psum x1, waiting for transfers between devices, one_after_other(): inner = lax.psum(x, axis_one)  86.3 us
    reduce_scatter x1, waiting for transfers between devices, shards(): lax.psum_scatter(part.astype(jnp.float32).astype(jnp.bfloat16), 'blk', sc...  39.3 us
    all_gather x1, waiting for transfers between devices, shards(): grouped = lax.all_gather(tokens, 'blk', axis=0, tiled=True)  35.9 us
    dot_general x1, matrix products, shards(): part = jnp.dot(hidden, down_full, preferred_element_type=jnp.float32)  29.6 us
    psum x1, blocking collectives, one_after_other(): return lax.psum(inner, axis_two)  20.1 us
  transfers between devices with their start and end apart: 6, of which 6 were waited for; matrix products, arithmetic and copies ran while one was open for 7% of the time, Pallas kernels for 0%

profile of v1, /device:TPU:0, one launch (start us, length us, event | category | flops | bytes accessed | tf_op | source)
XLA Modules:
  0.0 761.4 jit_solution(6306874284016280683)
XLA Ops:
  7.2 0.9 slice_bitcast_fusion.1
  8.1 1.7 select_reduce_fusion
  9.9 0.7 convert_element_type.34
  10.6 2.0 fusion.2
  12.6 2.7 convolution_bitcast_fusion
  15.3 1.8 fusion.4
  17.2 0.7 all-gather.4.cloned.1.call-update
  17.9 0.7 all-gather.8.cloned.1.call-update
  19.2 86.3 %all-reduce.7.cloned.1.call-done = (f32[4096,128]{0,1:T(8,128)}, f32[128,4096]{1,0:T(8,128)}) async-done(((f32[4096,128]{0,1:T(8,128)}, f32[128,4096]{1,0:T(8,128)}), (f32[4096,128]{0,1:T(8,128)}, f32[128,4096]{1,0:T(8,128)})) %all-reduce.7.cloned.1.call-update) | async-done | bytes 4194320 | tf_op jit(solution)/shard_map/psum | solution.py:8
  105.8 35.9 %all-gather.4.cloned.1.call-done = bf16[512,4096]{1,0:T(8,128)(2,1)} async-done(((bf16[128,4096]{1,0:T(8,128)(2,1)}), bf16[512,4096]{1,0:T(8,128)(2,1)}) %all-gather.4.cloned.1.call-update) | async-done | bytes 4194320 | tf_op jit(solution)/shard_map/all_gather | solution.py:24
  141.7 14.5 %fusion.12 = f32[512,1792]{1,0:T(8,128)} fusion(bf16[512,4096]{1,0:T(8,128)(2,1)} %all-gather.4.cloned.1.call-done, bf16[4096,1792]{1,0:T(8,128)(2,1)} %param.11), kind=kOutput, calls=%fused_computation.28 | convolution fusion | flops 7516192768 | bytes 22544384 | tf_op jit(solution)/shard_map/dot_general | solution.py:25
  156.2 189.3 %all-gather.8.cloned.1.call-done = bf16[1792,4096]{1,0:T(8,128)(2,1)} async-done(((bf16[1792,512]{1,0:T(8,128)(2,1)}), bf16[1792,4096]{1,0:T(8,128)(2,1)}) %all-gather.8.cloned.1.call-update) | async-done | bytes 14680080 | tf_op jit(solution)/shard_map/all_gather | solution.py:31
  345.5 201.9 %all-gather.6.cloned.1.call-done = bf16[4096,1792]{1,0:T(8,128)(2,1)} async-done(((bf16[512,1792]{1,0:T(8,128)(2,1)}), bf16[4096,1792]{1,0:T(8,128)(2,1)}) %all-gather.6.cloned.1.call-update) | async-done | bytes 14680080 | tf_op jit(solution)/shard_map/all_gather | solution.py:28
  547.4 29.6 %convolution_convert_fusion = bf16[512,4096]{1,0:T(8,128)(2,1)} fusion(bf16[1792,4096]{1,0:T(8,128)(2,1)} %all-gather.8.cloned.1.call-done, f32[512,1792]{1,0:T(8,128)} %fusion.12, bf16[512,4096]{1,0:T(8,128)(2,1)} %all-gather.4.cloned.1.call-done, bf16[4096,1792]{1,0:T(8,128)(2,1)} %all-gather.6.cloned.1.call-done), kind=kOutput, calls=%fused_computation | convolution fusion | flops 15039987712 | bytes 41418752 | tf_op jit(solution)/shard_map/dot_general | solution.py:33
  577.0 0.6 copy-done.3
  577.7 0.6 convert_reduce_fusion
  578.3 6.8 psum.44
  585.1 20.1 %psum.45 = f32[]{:T(128)} all-reduce(f32[]{:T(128)} %psum.44), channel_id=1, replica_groups=mesh['dp'=8,'blk'=4] {'dp'}, use_global_device_ids=true, to_apply=%region_7.8 | all-reduce | flops 1 | bytes 8 | tf_op jit(solution)/shard_map/psum | solution.py:9
  605.9 100.0 %all-reduce.5.cloned.1.call-done = (f32[4096,128]{0,1:T(8,128)}, f32[128,4096]{1,0:T(8,128)}) async-done(((f32[4096,128]{0,1:T(8,128)}, f32[128,4096]{1,0:T(8,128)}), (f32[4096,128]{0,1:T(8,128)}, f32[128,4096]{1,0:T(8,128)})) %all-reduce.5.cloned.1.call-update) | async-done | bytes 4194320 | tf_op jit(solution)/shard_map/psum | solution.py:9
  705.9 1.8 broadcast_multiply_fusion.1
  707.7 1.8 copy.16
  709.5 3.1 broadcast_multiply_fusion
  712.6 39.3 %reduce-scatter.2.cloned.1.call-done = bf16[128,4096]{1,0:T(8,128)(2,1)} async-done(((bf16[512,4096]{1,0:T(8,128)(2,1)}), bf16[128,4096]{1,0:T(8,128)(2,1)}) %reduce-scatter.2.cloned.1.call-update) | async-done | bytes 1048592 | tf_op jit(solution)/shard_map/reduce_scatter | solution.py:35
  751.9 2.6 fusion
  (21 shorter events, 1.1 us)
Async XLA Ops:
  7.2 5.4 copy-start
  7.2 5.4 copy-start.1
  7.2 5.4 copy-start.2
  7.2 98.3 %all-reduce.7.cloned.1.call-start = ((), (), s32[]{:S(2)}) async-start(), calls=%async_computation.6 | async-start | bytes 8388608 | tf_op jit(solution)/shard_map/psum | solution.py:8
  17.1 124.6 %all-gather.4.cloned.1.call-start = ((), (), s32[]{:S(2)}) async-start(), calls=%async_computation.1 | async-start | bytes 5242880 | tf_op jit(solution)/shard_map/all_gather | solution.py:24
  17.9 327.6 %all-gather.8.cloned.1.call-start = ((), (), s32[]{:S(2)}) async-start(), calls=%async_computation.3 | async-start | bytes 16515072 | tf_op jit(solution)/shard_map/all_gather | solution.py:31
  18.6 528.8 %all-gather.6.cloned.1.call-start = ((), (), s32[]{:S(2)}) async-start(), calls=%async_computation.2 | async-start | bytes 16515072 | tf_op jit(solution)/shard_map/all_gather | solution.py:28
  19.2 686.7 %all-reduce.5.cloned.1.call-start = ((), (), s32[]{:S(2)}) async-start(), calls=%async_computation.5 | async-start | bytes 8388608 | tf_op jit(solution)/shard_map/psum | solution.py:9
  105.5 646.4 %reduce-scatter.2.cloned.1.call-start = ((), (), s32[]{:S(2)}) async-start(), calls=%async_computation.4 | async-start | bytes 5242880 | tf_op jit(solution)/shard_map/reduce_scatter | solution.py:35
  577.0 0.7 copy-start.3
Sparse Core Ops, SparseCore 0:
  17.2 88.2 all-reduce.6
  107.1 34.5 all-gather.3
  143.8 201.7 all-gather.7
  347.6 199.8 all-gather.5
  551.0 154.8 all-reduce.4
  708.3 43.5 reduce-scatter.1
